TPU v7x, 32 devices: a whole 2x2x4 slice. The times are simulated.
32 devices in a mesh: tm: 4 (over y, x), paths: 8 (over z, core).
Axes of the slice: x: 2, y: 2, z: 4, core: 2. Of those that a mesh axis runs over, the one named last changes fastest.
Arguments:
- returns: bfloat16 [128, 4096, 256], P('tm', 'paths'), may hold values from -0.15917969 to 0.15917969
- weights: bfloat16 [256, 64], P('paths'), may hold values from -0.375 to 0.375
Outputs:
- drawdown: float32 [64, 4096], P('tm', 'paths')
All inputs are finite; a program needn't handle non-finite values.
Results may differ from a plain program's by a relative error of at most 0.0003.
Values may be sent and summed in bfloat16 or wider, within the bound.
A program may use at most 64 MiB of HBM per device.

v0:
```python
import jax
import jax.numpy as jnp
from jax import lax
from jax.sharding import PartitionSpec as P

very_large = 1e30


def prefix(part, axis, combine, identity):
    place = lax.axis_index(axis)
    gathered = jax.tree.map(lambda a: lax.all_gather(a, axis), part)
    state = jax.tree.map(lambda a, e: jnp.zeros_like(a) + jnp.asarray(e, a.dtype), part, identity)

    def one(lap, state):
        return combine(
            state, jax.tree.map(lambda a: lax.dynamic_index_in_dim(a, lap, 0, False), gathered)
        )

    return lax.fori_loop(0, place, one, state)


def join_two(earlier, later):
    return (earlier[0] + later[0], jnp.maximum(earlier[1], earlier[0] + later[1]))


def shards(returns, weights):
    all_weights = lax.all_gather(weights, "paths", axis=0, tiled=True)
    profit = jnp.einsum("tpa,aq->tqp", returns, all_weights, preferred_element_type=jnp.float32)
    steps_here = profit.shape[0]
    row_ids = lax.broadcasted_iota(jnp.int32, (steps_here, steps_here), 0)
    col_ids = lax.broadcasted_iota(jnp.int32, (steps_here, steps_here), 1)
    lower = (row_ids >= col_ids).astype(jnp.float32)
    flat = profit.reshape(steps_here, -1)
    values = jnp.dot(
        lower, flat, precision=lax.Precision.HIGHEST, preferred_element_type=jnp.float32
    ).reshape(profit.shape)
    peaks = jnp.maximum(lax.cummax(values, axis=0), 0.0)
    offset = values[-1]
    highest = peaks[-1]
    segments = lax.axis_size("tm")
    block_width = offset.shape[0] // segments
    zeros = jnp.zeros_like(offset)
    prior_offset, prior_peak = prefix(
        (offset, highest), "tm", join_two, (zeros, zeros - very_large)
    )
    running = jnp.maximum(prior_peak[None], prior_offset[None] + peaks)
    falls = jnp.max(running - (prior_offset[None] + values), axis=0)
    blocks = falls.reshape(segments, block_width, falls.shape[1])
    received = lax.all_to_all(blocks, "tm", split_axis=0, concat_axis=0, tiled=True)
    return jnp.max(received, axis=0)


def solution(mesh):
    in_specs = (P("tm", "paths", None), P("paths", None))
    out_specs = P("tm", "paths")
    return jax.shard_map(shards, mesh=mesh, in_specs=in_specs, out_specs=out_specs, check_vma=False)
```

profile of v0, /device:TPU:0, one launch (start us, length us, event | category | flops | bytes accessed | tf_op | source)
XLA Modules:
  0.0 87.8 jit_solution(8947005105098982368)
XLA Ops:
  0.0 15.9 %all_gather.9 = bf16[256,64]{1,0:T(8,128)(2,1)S(1)} all-gather(bf16[32,64]{1,0:T(8,128)(2,1)} %param.5), channel_id=1, replica_groups=mesh['tm'=4,'paths'=8] {'paths'}, dimensions={0}, use_global_device_ids=true | all-gather | bytes 36864 | tf_op jit(solution)/shard_map/all_gather | solution.py:27
  15.9 6.0 %fusion.1 = f32[64,32,512]{2,0,1:T(8,128)S(1)} fusion(bf16[32,512,256]{2,1,0:T(8,128)(2,1)} %param.4, bf16[256,64]{1,0:T(8,128)(2,1)S(1)} %all_gather.9), kind=kOutput, calls=%fused_computation.6 | convolution fusion | flops 536870912 | bytes 12615680 | tf_op jit(solution)/shard_map/tpa,aq->tqp/dot_general | solution.py:28
  21.9 2.4 %copy.3 = f32[4,8,64,512]{3,1,2,0:T(8,128)S(1)} copy(f32[4,8,64,512]{3,2,1,0:T(8,128)S(1)} %bitcast.27) | data formatting | bytes 8388608
  24.4 2.1 %fusion.3 = f32[32,32768]{1,0:T(8,128)S(1)} fusion(f32[32,32768]{1,0:T(8,128)S(1)} %bitcast.29), kind=kOutput, calls=%fused_computation.9 | convolution fusion | flops 402654208 | bytes 8388608 | tf_op jit(solution)/shard_map/dot_general | solution.py:34
  26.5 0.0 copy-start
  26.5 0.4 slice_reduce_fusion
  26.9 2.4 %copy.4 = f32[4,8,64,512]{3,2,1,0:T(8,128)S(1)} copy(f32[4,8,64,512]{3,1,2,0:T(8,128)S(1)} %bitcast.25) | data formatting | bytes 8388608
  29.3 0.0 copy-done
  29.3 20.9 %broadcast_maximum_fusion = f32[32,64,512]{2,1,0:T(8,128)S(1)} fusion(f32[32,64,512]{2,1,0:T(8,128)S(1)} %bitcast.30), kind=kOutput, calls=%fused_computation.4 | output fusion | flops 33554432 | bytes 8388608 | tf_op jit(solution)/shard_map/shards/reduce_window_max | solution.py:37
  50.2 0.0 copy-start.2
  50.2 2.0 %copy-done.2 = f32[32,64,512]{2,1,0:T(8,128)} copy-done((f32[32,64,512]{2,1,0:T(8,128)}, f32[32,64,512]{2,1,0:T(8,128)S(1)}, u32[]{:S(2)}) %copy-start.2) | copy-done | bytes 4194328
  52.2 10.3 %all_gather.11 = f32[4,64,512]{2,1,0:T(8,128)S(1)} all-gather(f32[1,64,512]{2,1,0:T(8,128)S(1)} %slice.13), channel_id=1, replica_groups=mesh['tm'=4,'paths'=8] {'tm'}, dimensions={0}, use_global_device_ids=true | all-gather | bytes 655360 | tf_op jit(solution)/shard_map/all_gather | solution.py:11
  62.6 10.7 %all_gather.10 = f32[4,64,512]{2,1,0:T(8,128)S(1)} all-gather(f32[1,64,512]{2,1,0:T(8,128)S(1)} %slice.10), channel_id=1, replica_groups=mesh['tm'=4,'paths'=8] {'tm'}, dimensions={0}, use_global_device_ids=true | all-gather | bytes 655360 | tf_op jit(solution)/shard_map/all_gather | solution.py:11
  73.3 0.2 while.12
  73.6 0.0 copy-start.1
  73.6 4.8 %copy.7 = f32[4,8,64,512]{3,1,2,0:T(8,128)S(1)} copy(f32[4,8,64,512]{3,2,1,0:T(8,128)} %bitcast.26) | data formatting | bytes 8388608
  78.4 0.0 copy-done.1
  78.4 0.9 %subtract_reduce_fusion = f32[32768]{0:T(1024)S(1)} fusion(f32[32,32768]{1,0:T(8,128)S(1)} %copy-done.1, f32[32,32768]{1,0:T(8,128)S(1)} %bitcast.28, f32[32768]{0:T(1024)S(1)} %bitcast.33, f32[32768]{0:T(1024)S(1)} %bitcast.34), kind=kLoop, calls=%fused_computation.3 | loop fusion | flops 5210112 | bytes 8781824 | tf_op jit(solution)/shard_map/reduce_max | solution.py:47
  79.4 7.8 %all_to_all.5 = f32[4,16,512]{2,1,0:T(8,128)S(1)} all-to-all(f32[4,16,512]{2,1,0:T(8,128)S(1)} %reshape.24), channel_id=1, replica_groups=mesh['tm'=4,'paths'=8] {'tm'}, dimensions={0} | all-to-all | bytes 262144 | tf_op jit(solution)/shard_map/all_to_all | solution.py:49
  87.2 0.6 reduce_max.19
  (7 shorter events, 0.1 us)
Async XLA Ops:
  26.5 2.8 %copy-start = (f32[32,32768]{1,0:T(8,128)}, f32[32,32768]{1,0:T(8,128)S(1)}, u32[]{:S(2)}) copy-start(f32[32,32768]{1,0:T(8,128)S(1)} %fusion.3) | copy-start | bytes 12582916
  50.2 2.0 %copy-start.2 = (f32[32,64,512]{2,1,0:T(8,128)}, f32[32,64,512]{2,1,0:T(8,128)S(1)}, u32[]{:S(2)}) copy-start(f32[32,64,512]{2,1,0:T(8,128)S(1)} %broadcast_maximum_fusion) | copy-start | bytes 12582916
  73.6 4.8 %copy-start.1 = (f32[32,32768]{1,0:T(8,128)S(1)}, f32[32,32768]{1,0:T(8,128)}, u32[]{:S(2)}) copy-start(f32[32,32768]{1,0:T(8,128)} %copy-done) | copy-start | bytes 12582916
where the time goes:
time: 88.1 us; the launch traced here: 87.8 us
  blocking collectives  44.8 us (51%)
  other arithmetic  22.5 us (26%)
  local copies, waits for them, and re-layouts  12.1 us (14%)
  matrix products  8.14 us (9%)
    all_gather x2, blocking collectives, prefix(): gathered = jax.tree.map(lambda a: lax.all_gather(a, axis), part)  21 us
    another operation x1, other arithmetic, shards(): peaks = jnp.maximum(lax.cummax(values, axis=0), 0.0)  20.9 us
    all_gather x1, blocking collectives, shards(): all_weights = lax.all_gather(weights, 'paths', axis=0, tiled=True)  15.9 us
    unnamed x11, local copies, waits for them, and re-layouts  11.7 us
    all_to_all x1, blocking collectives, shards(): lax.all_to_all(blocks, 'tm', split_axis=0, concat_axis=0, tiled=True)  7.85 us
    dot_general x1, matrix products, shards(): jnp.einsum('tpa,aq->tqp', returns, all_weights, preferred_element_type=jn...  6.03 us
    dot_general x1, matrix products, shards(): jnp.dot(lower, flat, precision=lax.Precision.HIGHEST, preferred_element_t...  2.11 us

commit v1 on v0

--- a/solution.py
+++ b/solution.py
@@ -24,8 +24,24 @@
 
 
 def shards(returns, weights):
-    all_weights = lax.all_gather(weights, "paths", axis=0, tiled=True)
-    profit = jnp.einsum("tpa,aq->tqp", returns, all_weights, preferred_element_type=jnp.float32)
+    then, arr_now = (jax.lax.axis_size("paths"), jax.lax.axis_index("paths"))
+    entries = [(u, (u - 1) % then) for u in range(then)]
+    y1 = weights.shape[0]
+    spare = weights
+    profit = jnp.einsum(
+        "tpa,aq->tqp",
+        lax.dynamic_slice_in_dim(returns, arr_now * y1, spare.shape[0], axis=2),
+        spare,
+        preferred_element_type=jnp.float32,
+    )
+    for at in range(1, then):
+        spare = jax.lax.ppermute(spare, "paths", entries)
+        profit = profit + jnp.einsum(
+            "tpa,aq->tqp",
+            lax.dynamic_slice_in_dim(returns, (arr_now + at) % then * y1, spare.shape[0], axis=2),
+            spare,
+            preferred_element_type=jnp.float32,
+        )
     steps_here = profit.shape[0]
     row_ids = lax.broadcasted_iota(jnp.int32, (steps_here, steps_here), 0)
     col_ids = lax.broadcasted_iota(jnp.int32, (steps_here, steps_here), 1)

time: 88.1 us -> 120 us (1.36)
  matrix products: 8.14 us -> 42.5 us
  blocking collectives: 44.8 us -> 28.6 us
  starting transfers between devices: 0 us -> 11.5 us
  local copies, waits for them, and re-layouts: 12.1 us -> 14.3 us
    dot_general x1 -> x8, matrix products: 6.03 us -> 40.4 us  [the longest x7 34.9 us: shards(): jnp.einsum('tpa,aq->tqp', lax.dynamic_slice_in_dim(returns, (arr_now + at...]
    all_gather x1 -> x0, blocking collectives: 15.9 us -> none  [shards(): all_weights = lax.all_gather(weights, 'paths', axis=0, tiled=True)]
    ppermute x0 -> x7, starting transfers between devices: none -> 11.5 us  [shards(): spare = jax.lax.ppermute(spare, 'paths', entries)]
    unnamed x11 -> x13, local copies, waits for them, and re-layouts: 11.7 us -> 13.9 us
  transfers between devices with their start and end apart: 0 -> 7, of which waited for: 0 -> 0; matrix products, arithmetic and copies ran while one was open for 0% -> 23% of each run, Pallas kernels for 0% -> 0%
where the time goes in v1:
time: 120 us
  matrix products  42.5 us (35%)
  blocking collectives  28.6 us (24%)
  other arithmetic  22.5 us (19%)
  local copies, waits for them, and re-layouts  14.3 us (12%)
  starting transfers between devices  11.5 us (10%)
    dot_general x7, matrix products, shards(): jnp.einsum('tpa,aq->tqp', lax.dynamic_slice_in_dim(returns, (arr_now + at...  34.9 us
    another operation x1, other arithmetic, shards(): peaks = jnp.maximum(lax.cummax(values, axis=0), 0.0)  20.9 us
    all_gather x2, blocking collectives, prefix(): gathered = jax.tree.map(lambda a: lax.all_gather(a, axis), part)  20.8 us
    unnamed x13, local copies, waits for them, and re-layouts  13.9 us
    ppermute x7, starting transfers between devices, shards(): spare = jax.lax.ppermute(spare, 'paths', entries)  11.5 us
    all_to_all x1, blocking collectives, shards(): lax.all_to_all(blocks, 'tm', split_axis=0, concat_axis=0, tiled=True)  7.85 us
    dot_general x1, matrix products, shards(): jnp.einsum('tpa,aq->tqp', lax.dynamic_slice_in_dim(returns, arr_now * y1,...  5.46 us
  transfers between devices with their start and end apart: 7, of which 0 were waited for; matrix products, arithmetic and copies ran while one was open for 23% of the time, Pallas kernels for 0%

profile of v1, /device:TPU:0, one launch (start us, length us, event | category | flops | bytes accessed | tf_op | source)
XLA Modules:
  0.0 119.8 jit_solution(18070147842172265604)
XLA Ops:
  0.0 4.5 %collective-permute-start = (bf16[32,64]{1,0:T(8,128)(2,1)}, bf16[32,64]{1,0:T(8,128)(2,1)S(1)}, u32[]{:S(2)}, u32[]{:S(2)}) collective-permute-start(bf16[32,64]{1,0:T(8,128)(2,1)} %param.5), channel_id=1, source_target_pairs={{0,7},{1,0},{2,1},{3,2},{4,3},{5,4},{6,5},{7,6},{8,15},{9,8},{10,9... | collective-permute-start | bytes 12296 | tf_op jit(solution)/shard_map/ppermute | solution.py:38
  4.5 5.5 %fusion.15 = f32[32,512,64]{1,2,0:T(8,128)} fusion(bf16[32,512,256]{2,1,0:T(8,128)(2,1)} %param.4, s32[]{:T(128)S(6)} %select_n.60, bf16[32,64]{1,0:T(8,128)(2,1)} %param.5), kind=kOutput, calls=%fused_computation.19 | convolution fusion | flops 67108864 | bytes 8396804 | tf_op jit(solution)/shard_map/tpa,aq->tqp/dot_general | solution.py:31
  10.0 0.0 copy-start
  10.0 0.0 collective-permute-done
  10.0 0.7 collective-permute-start.1
  10.7 5.8 %fusion.13 = f32[32,512,64]{1,2,0:T(8,128)} fusion(bf16[32,512,256]{2,1,0:T(8,128)(2,1)} %param.4, s32[]{:T(128)S(6)} %select_n.62, bf16[32,64]{1,0:T(8,128)(2,1)S(1)} %collective-permute-done), kind=kOutput, calls=%fused_computation.17 | convolution fusion | flops 67108864 | bytes 8392708 | tf_op jit(solution)/shard_map/tpa,aq->tqp/dot_general | solution.py:39
  16.4 0.0 collective-permute-done.1
  16.4 0.0 collective-permute-start.2
  16.4 0.0 copy-done
  16.4 3.3 %fusion.11 = f32[32,512,64]{1,2,0:T(8,128)} fusion(bf16[32,512,256]{2,1,0:T(8,128)(2,1)S(1)} %copy-done, s32[]{:T(128)S(6)} %select_n.64, bf16[32,64]{1,0:T(8,128)(2,1)S(1)} %collective-permute-done.1), kind=kOutput, calls=%fused_computation.15 | convolution fusion | flops 67108864 | bytes 8396804 | tf_op jit(solution)/shard_map/tpa,aq->tqp/dot_general | solution.py:39
  19.7 0.0 collective-permute-done.2
  19.7 1.6 %collective-permute-start.3 = (bf16[32,64]{1,0:T(8,128)(2,1)S(1)}, bf16[32,64]{1,0:T(8,128)(2,1)S(1)}, u32[]{:S(2)}, u32[]{:S(2)}) collective-permute-start(bf16[32,64]{1,0:T(8,128)(2,1)S(1)} %collective-permute-done.2), channel_id=1, source_target_pairs={{0,7},{1,0},{2,1},{3,2},{4,3},{5,4},{6,5},{7,6},{8,15},{9,8},{10,9... | collective-permute-start | bytes 12296 | tf_op jit(solution)/shard_map/ppermute | solution.py:38
  21.3 3.3 %fusion.9 = f32[32,512,64]{1,2,0:T(8,128)} fusion(bf16[32,512,256]{2,1,0:T(8,128)(2,1)S(1)} %copy-done, s32[]{:T(128)S(6)} %select_n.66, bf16[32,64]{1,0:T(8,128)(2,1)S(1)} %collective-permute-done.2), kind=kOutput, calls=%fused_computation.13 | convolution fusion | flops 67108864 | bytes 8396804 | tf_op jit(solution)/shard_map/tpa,aq->tqp/dot_general | solution.py:39
  24.6 0.0 collective-permute-done.3
  24.6 1.6 %collective-permute-start.4 = (bf16[32,64]{1,0:T(8,128)(2,1)S(1)}, bf16[32,64]{1,0:T(8,128)(2,1)S(1)}, u32[]{:S(2)}, u32[]{:S(2)}) collective-permute-start(bf16[32,64]{1,0:T(8,128)(2,1)S(1)} %collective-permute-done.3), channel_id=1, source_target_pairs={{0,7},{1,0},{2,1},{3,2},{4,3},{5,4},{6,5},{7,6},{8,15},{9,8},{10,9... | collective-permute-start | bytes 12296 | tf_op jit(solution)/shard_map/ppermute | solution.py:38
  26.2 3.3 %fusion.7 = f32[32,512,64]{1,2,0:T(8,128)} fusion(bf16[32,512,256]{2,1,0:T(8,128)(2,1)S(1)} %copy-done, s32[]{:T(128)S(6)} %select_n.68, bf16[32,64]{1,0:T(8,128)(2,1)S(1)} %collective-permute-done.3), kind=kOutput, calls=%fused_computation.11 | convolution fusion | flops 67108864 | bytes 8396804 | tf_op jit(solution)/shard_map/tpa,aq->tqp/dot_general | solution.py:39
  29.5 0.0 collective-permute-done.4
  29.5 1.6 %collective-permute-start.5 = (bf16[32,64]{1,0:T(8,128)(2,1)S(1)}, bf16[32,64]{1,0:T(8,128)(2,1)S(1)}, u32[]{:S(2)}, u32[]{:S(2)}) collective-permute-start(bf16[32,64]{1,0:T(8,128)(2,1)S(1)} %collective-permute-done.4), channel_id=1, source_target_pairs={{0,7},{1,0},{2,1},{3,2},{4,3},{5,4},{6,5},{7,6},{8,15},{9,8},{10,9... | collective-permute-start | bytes 12296 | tf_op jit(solution)/shard_map/ppermute | solution.py:38
  31.1 3.3 %fusion.5 = f32[32,512,64]{1,2,0:T(8,128)} fusion(bf16[32,512,256]{2,1,0:T(8,128)(2,1)S(1)} %copy-done, s32[]{:T(128)S(6)} %select_n.70, bf16[32,64]{1,0:T(8,128)(2,1)S(1)} %collective-permute-done.4), kind=kOutput, calls=%fused_computation.9 | convolution fusion | flops 67108864 | bytes 8396804 | tf_op jit(solution)/shard_map/tpa,aq->tqp/dot_general | solution.py:39
  34.4 0.0 collective-permute-done.5
  34.4 1.6 %collective-permute-start.6 = (bf16[32,64]{1,0:T(8,128)(2,1)S(1)}, bf16[32,64]{1,0:T(8,128)(2,1)S(1)}, u32[]{:S(2)}, u32[]{:S(2)}) collective-permute-start(bf16[32,64]{1,0:T(8,128)(2,1)S(1)} %collective-permute-done.5), channel_id=1, source_target_pairs={{0,7},{1,0},{2,1},{3,2},{4,3},{5,4},{6,5},{7,6},{8,15},{9,8},{10,9... | collective-permute-start | bytes 12296 | tf_op jit(solution)/shard_map/ppermute | solution.py:38
  35.9 3.3 %fusion.3 = f32[32,512,64]{1,2,0:T(8,128)} fusion(bf16[32,512,256]{2,1,0:T(8,128)(2,1)S(1)} %copy-done, s32[]{:T(128)S(6)} %select_n.72, bf16[32,64]{1,0:T(8,128)(2,1)S(1)} %collective-permute-done.5), kind=kOutput, calls=%fused_computation.7 | convolution fusion | flops 67108864 | bytes 8396804 | tf_op jit(solution)/shard_map/tpa,aq->tqp/dot_general | solution.py:39
  39.2 0.0 collective-permute-done.6
  39.2 12.7 %add_add_fusion = f32[32,512,64]{1,2,0:T(8,128)} fusion(f32[32,512,64]{1,2,0:T(8,128)} %fusion.3, f32[32,512,64]{1,2,0:T(8,128)} %fusion.5, f32[32,512,64]{1,2,0:T(8,128)} %fusion.7, f32[32,512,64]{1,2,0:T(8,128)} %fusion.9, f32[32,512,64]{1,2,0:T(8,128)} %fusion.11, f32[32,512,64]{1,2,0:T(8,128)} %fusion.15, f32[32,512,64]{1,2,0:T(8,128)} %fusion.13, ...), kind=kOutput, calls=%fused_computation.3 | convolution fusion | flops 74448896 | bytes 37756932 | tf_op jit(solution)/shard_map/tpa,aq->tqp/dot_general | solution.py:39
  52.0 4.6 %copy.35 = f32[4,8,64,512]{3,1,2,0:T(8,128)S(1)} copy(f32[4,8,64,512]{3,2,1,0:T(8,128)} %bitcast.50) | data formatting | bytes 8388608
  56.6 2.1 %fusion.19 = f32[32,32768]{1,0:T(8,128)S(1)} fusion(f32[32,32768]{1,0:T(8,128)S(1)} %bitcast.48), kind=kOutput, calls=%fused_computation.24 | convolution fusion | flops 402654208 | bytes 8388608 | tf_op jit(solution)/shard_map/dot_general | solution.py:50
  58.7 0.0 copy-start.1
  58.7 0.4 slice_reduce_fusion
  59.1 2.4 %copy.36 = f32[4,8,64,512]{3,2,1,0:T(8,128)S(1)} copy(f32[4,8,64,512]{3,1,2,0:T(8,128)S(1)} %bitcast.45) | data formatting | bytes 8388608
  61.5 0.0 copy-done.1
  61.5 20.9 %broadcast_maximum_fusion = f32[32,64,512]{2,1,0:T(8,128)S(1)} fusion(f32[32,64,512]{2,1,0:T(8,128)S(1)} %bitcast.49), kind=kOutput, calls=%fused_computation.21 | output fusion | flops 33554432 | bytes 8388608 | tf_op jit(solution)/shard_map/shards/reduce_window_max | solution.py:53
  82.5 0.0 copy-start.3
  82.5 2.0 %copy-done.3 = f32[32,64,512]{2,1,0:T(8,128)} copy-done((f32[32,64,512]{2,1,0:T(8,128)}, f32[32,64,512]{2,1,0:T(8,128)S(1)}, u32[]{:S(2)}) %copy-start.3) | copy-done | bytes 4194328
  84.4 10.0 %all_gather.7 = f32[4,64,512]{2,1,0:T(8,128)S(1)} all-gather(f32[1,64,512]{2,1,0:T(8,128)S(1)} %slice.13), channel_id=1, replica_groups=mesh['tm'=4,'paths'=8] {'tm'}, dimensions={0}, use_global_device_ids=true | all-gather | bytes 655360 | tf_op jit(solution)/shard_map/all_gather | solution.py:11
  94.5 10.7 %all_gather.6 = f32[4,64,512]{2,1,0:T(8,128)S(1)} all-gather(f32[1,64,512]{2,1,0:T(8,128)S(1)} %slice.10), channel_id=1, replica_groups=mesh['tm'=4,'paths'=8] {'tm'}, dimensions={0}, use_global_device_ids=true | all-gather | bytes 655360 | tf_op jit(solution)/shard_map/all_gather | solution.py:11
  105.3 0.2 while.12
  105.6 0.0 copy-start.2
  105.6 4.8 %copy.39 = f32[4,8,64,512]{3,1,2,0:T(8,128)S(1)} copy(f32[4,8,64,512]{3,2,1,0:T(8,128)} %bitcast.46) | data formatting | bytes 8388608
  110.4 0.0 copy-done.2
  110.4 0.9 subtract_reduce_fusion
  111.3 7.9 %all_to_all.5 = f32[4,16,512]{2,1,0:T(8,128)S(1)} all-to-all(f32[4,16,512]{2,1,0:T(8,128)S(1)} %reshape.24), channel_id=1, replica_groups=mesh['tm'=4,'paths'=8] {'tm'}, dimensions={0} | all-to-all | bytes 262144 | tf_op jit(solution)/shard_map/all_to_all | solution.py:65
  119.2 0.6 reduce_max.19
  (7 shorter events, 0.1 us)
Async XLA Ops:
  0.0 10.0 %collective-permute-start = (bf16[32,64]{1,0:T(8,128)(2,1)}, bf16[32,64]{1,0:T(8,128)(2,1)S(1)}, u32[]{:S(2)}, u32[]{:S(2)}) collective-permute-start(bf16[32,64]{1,0:T(8,128)(2,1)} %param.5), channel_id=1, source_target_pairs={{0,7},{1,0},{2,1},{3,2},{4,3},{5,4},{6,5},{7,6},{8,15},{9,8},{10,9... | collective-permute-start | bytes 12296 | tf_op jit(solution)/shard_map/ppermute | solution.py:38
  10.0 6.5 %copy-start = (bf16[32,512,256]{2,1,0:T(8,128)(2,1)S(1)}, bf16[32,512,256]{2,1,0:T(8,128)(2,1)}, u32[]{:S(2)}) copy-start(bf16[32,512,256]{2,1,0:T(8,128)(2,1)} %param.4) | copy-start | bytes 25165828
  10.0 6.4 %collective-permute-start.1 = (bf16[32,64]{1,0:T(8,128)(2,1)S(1)}, bf16[32,64]{1,0:T(8,128)(2,1)S(1)}, u32[]{:S(2)}, u32[]{:S(2)}) collective-permute-start(bf16[32,64]{1,0:T(8,128)(2,1)S(1)} %collective-permute-done), channel_id=1, source_target_pairs={{0,7},{1,0},{2,1},{3,2},{4,3},{5,4},{6,5},{7,6},{8,15},{9,8},{10,9... | collective-permute-start | bytes 12296 | tf_op jit(solution)/shard_map/ppermute | solution.py:38
  16.4 3.3 %collective-permute-start.2 = (bf16[32,64]{1,0:T(8,128)(2,1)S(1)}, bf16[32,64]{1,0:T(8,128)(2,1)S(1)}, u32[]{:S(2)}, u32[]{:S(2)}) collective-permute-start(bf16[32,64]{1,0:T(8,128)(2,1)S(1)} %collective-permute-done.1), channel_id=1, source_target_pairs={{0,7},{1,0},{2,1},{3,2},{4,3},{5,4},{6,5},{7,6},{8,15},{9,8},{10,9... | collective-permute-start | bytes 12296 | tf_op jit(solution)/shard_map/ppermute | solution.py:38
  19.7 4.9 %collective-permute-start.3 = (bf16[32,64]{1,0:T(8,128)(2,1)S(1)}, bf16[32,64]{1,0:T(8,128)(2,1)S(1)}, u32[]{:S(2)}, u32[]{:S(2)}) collective-permute-start(bf16[32,64]{1,0:T(8,128)(2,1)S(1)} %collective-permute-done.2), channel_id=1, source_target_pairs={{0,7},{1,0},{2,1},{3,2},{4,3},{5,4},{6,5},{7,6},{8,15},{9,8},{10,9... | collective-permute-start | bytes 12296 | tf_op jit(solution)/shard_map/ppermute | solution.py:38
  24.6 4.9 %collective-permute-start.4 = (bf16[32,64]{1,0:T(8,128)(2,1)S(1)}, bf16[32,64]{1,0:T(8,128)(2,1)S(1)}, u32[]{:S(2)}, u32[]{:S(2)}) collective-permute-start(bf16[32,64]{1,0:T(8,128)(2,1)S(1)} %collective-permute-done.3), channel_id=1, source_target_pairs={{0,7},{1,0},{2,1},{3,2},{4,3},{5,4},{6,5},{7,6},{8,15},{9,8},{10,9... | collective-permute-start | bytes 12296 | tf_op jit(solution)/shard_map/ppermute | solution.py:38
  29.5 4.9 %collective-permute-start.5 = (bf16[32,64]{1,0:T(8,128)(2,1)S(1)}, bf16[32,64]{1,0:T(8,128)(2,1)S(1)}, u32[]{:S(2)}, u32[]{:S(2)}) collective-permute-start(bf16[32,64]{1,0:T(8,128)(2,1)S(1)} %collective-permute-done.4), channel_id=1, source_target_pairs={{0,7},{1,0},{2,1},{3,2},{4,3},{5,4},{6,5},{7,6},{8,15},{9,8},{10,9... | collective-permute-start | bytes 12296 | tf_op jit(solution)/shard_map/ppermute | solution.py:38
  34.4 4.9 %collective-permute-start.6 = (bf16[32,64]{1,0:T(8,128)(2,1)S(1)}, bf16[32,64]{1,0:T(8,128)(2,1)S(1)}, u32[]{:S(2)}, u32[]{:S(2)}) collective-permute-start(bf16[32,64]{1,0:T(8,128)(2,1)S(1)} %collective-permute-done.5), channel_id=1, source_target_pairs={{0,7},{1,0},{2,1},{3,2},{4,3},{5,4},{6,5},{7,6},{8,15},{9,8},{10,9... | collective-permute-start | bytes 12296 | tf_op jit(solution)/shard_map/ppermute | solution.py:38
  58.7 2.8 %copy-start.1 = (f32[32,32768]{1,0:T(8,128)}, f32[32,32768]{1,0:T(8,128)S(1)}, u32[]{:S(2)}) copy-start(f32[32,32768]{1,0:T(8,128)S(1)} %fusion.19) | copy-start | bytes 12582916
  82.5 2.0 %copy-start.3 = (f32[32,64,512]{2,1,0:T(8,128)}, f32[32,64,512]{2,1,0:T(8,128)S(1)}, u32[]{:S(2)}) copy-start(f32[32,64,512]{2,1,0:T(8,128)S(1)} %broadcast_maximum_fusion) | copy-start | bytes 12582916
  105.6 4.8 %copy-start.2 = (f32[32,32768]{1,0:T(8,128)S(1)}, f32[32,32768]{1,0:T(8,128)}, u32[]{:S(2)}) copy-start(f32[32,32768]{1,0:T(8,128)} %copy-done.1) | copy-start | bytes 12582916
